TPU v7x, 32 devices: a whole 2x2x4 slice. The times are simulated.
32 devices in a mesh: tm: 4 (over y, core), rows: 8 (over z, x).
Axes of the slice: x: 2, y: 2, z: 4, core: 2. Of those that a mesh axis runs over, the one named last changes fastest.
Arguments:
- features: bfloat16 [4, 24, 64, 512], P('tm', 'rows'), may hold values from -64 to 64, as said below
- gamma: float32 [512], replicated, may hold values from 0.1 to 1.9
- beta: float32 [512], replicated, may hold values from -3 to 3
- kernel: bfloat16 [3, 512, 3, 3, 512], P(None, 'tm'), may hold values from -0.0546875 to 0.0546875
- bias: float32 [512], replicated, may hold values from -3 to 3
Outputs:
- decoded: bfloat16 [4, 24, 64, 512], P('tm', 'rows')
Inputs may be any that keep to these rules, and one draw needn't show every extreme that they name: features are finite.
All inputs are finite; a program needn't handle non-finite values.
Results may differ from a plain program's by a relative error of at most 0.004.
Values may be sent and summed in bfloat16 or wider, within the bound.
A program may use at most 128 MiB of HBM per device.

v0:
```python
import jax
import jax.numpy as jnp
from jax import lax
from jax.sharding import PartitionSpec as P

GROUPS = 32
EPSILON = 1e-06


def shifted(x, axis, by):
    length = lax.axis_size(axis)
    pairs = [(i, i + by) for i in range(length) if 0 <= i + by < length]
    return lax.ppermute(x, axis, pairs)


def extended_2(x, sides, width):
    for axis, dim in sides:
        size, length = (lax.axis_size(axis), x.shape[dim])
        up = [(i, (i + 1) % size) for i in range(size - 1)]
        down = [(j, i) for i, j in up]
        last = lax.slice_in_dim(x, length - width, length, axis=dim)
        first = lax.slice_in_dim(x, 0, width, axis=dim)
        before = lax.ppermute(last, axis, up)
        after = lax.ppermute(first, axis, down)
        x = jnp.concatenate([before, x, after], axis=dim)
    return x


def unfold(block, height, across):
    pieces = []
    for tap_row in range(3):
        for tap_col in range(3):
            pieces.append(block[:, tap_row : tap_row + height, tap_col : tap_col + across, :])
    return jnp.concatenate(pieces, axis=-1)


def flatten_taps(taps):
    return taps.reshape(3, taps.shape[1], -1)


def apply_taps(columns, taps, frames):
    flat = flatten_taps(taps)
    total = jnp.einsum(
        "fhwc,kc->fhwk", columns[0:frames], flat[0], preferred_element_type=jnp.float32
    )
    for tap_time in (1, 2):
        total = total + jnp.einsum(
            "fhwc,kc->fhwk",
            columns[tap_time : tap_time + frames],
            flat[tap_time],
            preferred_element_type=jnp.float32,
        )
    return total


def widen(block):
    return jnp.pad(block, ((0, 0), (0, 0), (1, 1), (0, 0)))


def previous_span(block):
    return shifted(block, "tm", 1)


def local(features, gamma, beta, kernel, bias):
    frames, height, across, channels = features.shape
    values = features.astype(jnp.float32)
    grouped = values.reshape(frames, height, across, GROUPS, channels // GROUPS)
    count = float(
        frames
        * height
        * across
        * (channels // GROUPS)
        * lax.axis_size("tm")
        * lax.axis_size("rows")
    )
    totals, squares = lax.psum(
        (jnp.sum(grouped, axis=(0, 1, 2, 4)), jnp.sum(grouped * grouped, axis=(0, 1, 2, 4))),
        ("tm", "rows"),
    )
    center = totals / count
    spread = squares / count - center * center
    centered = grouped - center[:, None]
    normed = (centered * lax.rsqrt(spread + EPSILON)[:, None]).reshape(
        frames, height, across, channels
    )
    active = jax.nn.silu(normed * gamma + beta).astype(jnp.bfloat16)
    rimmed = extended_2(active, (("rows", 1),), 1)
    first_span = lax.axis_index("tm") == 0
    minus_one = jnp.where(first_span, rimmed, previous_span(rimmed))
    minus_two = jnp.where(first_span, rimmed, previous_span(minus_one))
    cache = jnp.concatenate([minus_two, minus_one], axis=0)
    extended = widen(jnp.concatenate([cache, rimmed], axis=0))
    columns = unfold(extended, height, across)
    conv = apply_taps(columns, lax.all_gather(kernel, "tm", axis=1, tiled=True), frames)
    return (values + conv + bias).astype(jnp.bfloat16)


def solution(mesh):
    in_specs = (P("tm", "rows", None, None), P(), P(), P(None, "tm", None, None, None), P())
    out_specs = P("tm", "rows", None, None)
    return jax.shard_map(local, mesh=mesh, in_specs=in_specs, out_specs=out_specs, check_vma=False)
```

profile of v0, /device:TPU:13, one launch (start us, length us, event | category | flops | bytes accessed | tf_op | source)
XLA Modules:
  0.0 135.2 jit_solution(9544178804054469499)
XLA Ops:
  6.5 0.0 copy-start
  6.5 0.0 copy-start.1
  6.5 0.0 copy-start.2
  6.5 0.0 all-gather.2.cloned.1.call-start
  6.5 6.1 %copy.9 = bf16[3,128,3,3,512]{1,4,3,2,0:T(8,128)(2,1)} copy(bf16[3,128,3,3,512]{4,1,3,2,0:T(8,128)(2,1)} %param.8) | data formatting | bytes 7077888 | tf_op args[3]
  12.6 0.0 all-gather.2.cloned.1.call-update
  12.6 0.0 copy-done
  12.6 0.1 convert_reduce_fusion
  12.7 0.1 reduce_sum.36
  12.8 0.1 reduce_sum.24
  12.9 0.1 reduce_sum.37
  13.0 0.1 reduce_sum.25
  13.1 40.4 %all-reduce.1 = (f32[32]{0:T(128)S(1)}, f32[32]{0:T(128)S(1)}) all-reduce(f32[32]{0:T(128)S(1)} %reduce_sum.37, f32[32]{0:T(128)S(1)} %reduce_sum.25), channel_id=1, replica_groups=mesh['tm'=4,'rows'=8] {'tm','rows'}, use_global_device_ids=true, to_apply=%region_5.6 | all-reduce | flops 64 | bytes 512 | tf_op jit(solution)/shard_map/psum | solution.py:76
  53.5 0.1 mul.43
  53.6 0.1 mul.44
  53.7 0.1 sub.19
  53.7 0.1 sub.20
  53.8 0.0 copy-done.1
  53.8 0.0 copy-done.2
  53.8 0.1 fusion.23
  54.0 3.0 %collective-permute-start.1 = (bf16[1,1,64,512]{3,2,1,0:T(8,128)(2,1)S(1)}, bf16[1,1,64,512]{3,2,1,0:T(8,128)(2,1)S(1)}, u32[]{:S(2)}, u32[]{:S(2)}) collective-permute-start(bf16[1,1,64,512]{3,2,1,0:T(8,128)(2,1)S(1)} %get-tuple-element.13), channel_id=1, source_target_pairs={{1,0},{2,1},{3,2},{4,3},{5,4},{6,5},{7,6},{9,8},{10,9},{11,10},{12... | collective-permute-start | bytes 196616 | tf_op jit(solution)/shard_map/ppermute | solution.py:24
  57.0 2.3 %collective-permute-start = (bf16[1,1,64,512]{3,2,1,0:T(8,128)(2,1)S(1)}, bf16[1,1,64,512]{3,2,1,0:T(8,128)(2,1)S(1)}, u32[]{:S(2)}, u32[]{:S(2)}) collective-permute-start(bf16[1,1,64,512]{3,2,1,0:T(8,128)(2,1)S(1)} %get-tuple-element.12), channel_id=1, source_target_pairs={{0,1},{1,2},{2,3},{3,4},{4,5},{5,6},{6,7},{8,9},{9,10},{10,11},{11... | collective-permute-start | bytes 196616 | tf_op jit(solution)/shard_map/ppermute | solution.py:23
  59.3 0.1 collective-permute-done.1
  59.4 3.5 %collective-permute-done = bf16[1,1,64,512]{3,2,1,0:T(8,128)(2,1)S(1)} collective-permute-done((bf16[1,1,64,512]{3,2,1,0:T(8,128)(2,1)S(1)}, bf16[1,1,64,512]{3,2,1,0:T(8,128)(2,1)S(1)}, u32[]{:S(2)}, u32[]{:S(2)}) %collective-permute-start) | collective-permute-done | bytes 65568 | tf_op jit(solution)/shard_map/ppermute | solution.py:23
  63.0 1.3 collective-permute-start.2
  64.3 5.3 %collective-permute-done.2 = bf16[1,5,64,512]{3,2,1,0:T(8,128)(2,1)S(1)} collective-permute-done((bf16[1,5,64,512]{3,2,1,0:T(8,128)(2,1)S(1)}, bf16[1,5,64,512]{3,2,1,0:T(8,128)(2,1)S(1)}, u32[]{:S(2)}, u32[]{:S(2)}) %collective-permute-start.2) | collective-permute-done | bytes 327712 | tf_op jit(solution)/shard_map/ppermute | solution.py:13
  69.7 1.3 collective-permute-start.3
  71.0 13.8 %collective-permute-done.3 = bf16[1,5,64,512]{3,2,1,0:T(8,128)(2,1)S(1)} collective-permute-done((bf16[1,5,64,512]{3,2,1,0:T(8,128)(2,1)S(1)}, bf16[1,5,64,512]{3,2,1,0:T(8,128)(2,1)S(1)}, u32[]{:S(2)}, u32[]{:S(2)}) %collective-permute-start.3) | collective-permute-done | bytes 327712 | tf_op jit(solution)/shard_map/ppermute | solution.py:13
  84.8 0.1 broadcast_select_fusion
  84.8 0.1 maximum_maximum_fusion
  84.9 1.0 fusion.9
  85.9 0.9 slice_dynamic-update-slice_fusion.2
  86.8 1.0 fusion.10
  87.8 1.0 fusion.11
  88.8 0.9 slice_dynamic-update-slice_fusion.1
  89.8 1.0 fusion.12
  90.8 1.0 fusion.13
  91.8 1.0 slice_dynamic-update-slice_fusion
  92.8 1.0 fusion.14
  93.8 20.4 %all-gather.2.cloned.1.call-done = bf16[3,512,3,3,512]{1,4,3,2,0:T(8,128)(2,1)} async-done(((bf16[3,128,3,3,512]{1,4,3,2,0:T(8,128)(2,1)}), bf16[3,512,3,3,512]{1,4,3,2,0:T(8,128)(2,1)}) %all-gather.2.cloned.1.call-update) | async-done | bytes 14155792 | tf_op jit(solution)/shard_map/all_gather | solution.py:94
  114.2 5.7 %fusion.25 = (bf16[1,512,3,3,512]{1,4,3,2,0:T(8,128)(2,1)S(1)}, bf16[1,512,3,3,512]{1,4,3,2,0:T(8,128)(2,1)S(1)}, bf16[1,512,3,3,512]{1,4,3,2,0:T(8,128)(2,1)S(1)}) fusion(bf16[3,512,3,3,512]{1,4,3,2,0:T(8,128)(2,1)} %all-gather.2.cloned.1.call-done), kind=kLoop, calls=%fused_computation.46 | loop fusion | bytes 28311552 | tf_op jit(solution)/shard_map/slice | solution.py:44
  120.0 2.5 %fusion = f32[3,64,512]{2,1,0:T(8,128)S(1)} fusion(bf16[512,4608,1]{0,1,2:T(8,128)(2,1)S(1)} %bitcast.43, bf16[3,3,64,4608]{3,2,1,0:T(8,128)(2,1)} %fusion.14), kind=kOutput, calls=%fused_computation.1 | convolution fusion | flops 905969664 | bytes 6881280 | tf_op jit(solution)/shard_map/fhwc,kc->fhwk/dot_general | solution.py:47
  122.5 0.0 copy-start.3
  122.5 2.6 %fusion.1 = f32[3,64,512]{2,1,0:T(8,128)S(1)} fusion(bf16[512,4608,1]{0,1,2:T(8,128)(2,1)S(1)} %bitcast.42, bf16[3,3,64,4608]{3,2,1,0:T(8,128)(2,1)} %fusion.14), kind=kOutput, calls=%fused_computation.3 | convolution fusion | flops 905969664 | bytes 6881280 | tf_op jit(solution)/shard_map/fhwc,kc->fhwk/dot_general | solution.py:47
  125.1 0.0 copy-done.3
  125.1 3.3 %fusion.8 = bf16[1,3,64,512]{3,2,1,0:T(8,128)(2,1)} fusion(f32[3,64,512]{2,1,0:T(8,128)S(1)} %fusion, f32[3,64,512]{2,1,0:T(8,128)S(1)} %fusion.1, bf16[512,4608,1]{0,1,2:T(8,128)(2,1)S(1)} %bitcast.41, bf16[3,3,64,4608]{3,2,1,0:T(8,128)(2,1)} %fusion.14, bf16[1,3,64,512]{3,2,1,0:T(8,128)(2,1)S(1)} %copy-done, f32[512]{0:T(512)S(1)} %copy-done.3), kind=kOutput, calls=%fused_computation.11 | convolution fusion | flops 906559488 | bytes 7669760 | tf_op jit(solution)/shard_map/fhwc,kc->fhwk/dot_general | solution.py:43
  (4 shorter events, 0.1 us)
Async XLA Ops:
  6.5 6.1 %copy-start = (bf16[1,3,64,512]{3,2,1,0:T(8,128)(2,1)S(1)}, bf16[1,3,64,512]{3,2,1,0:T(8,128)(2,1)}, u32[]{:S(2)}) copy-start(bf16[1,3,64,512]{3,2,1,0:T(8,128)(2,1)} %param.5) | copy-start | bytes 589828
  6.5 47.3 %copy-start.1 = (f32[512]{0:T(512)S(1)}, f32[512]{0:T(512)}, u32[]{:S(2)}) copy-start(f32[512]{0:T(512)} %param.7) | copy-start | bytes 6148
  6.5 47.3 %copy-start.2 = (f32[512]{0:T(512)S(1)}, f32[512]{0:T(512)}, u32[]{:S(2)}) copy-start(f32[512]{0:T(512)} %param.6) | copy-start | bytes 6148
  6.5 107.7 %all-gather.2.cloned.1.call-start = ((), (), s32[]{:S(2)}) async-start(), calls=%async_computation | async-start | bytes 17694720 | tf_op jit(solution)/shard_map/all_gather | solution.py:94
  54.0 5.4 %collective-permute-start.1 = (bf16[1,1,64,512]{3,2,1,0:T(8,128)(2,1)S(1)}, bf16[1,1,64,512]{3,2,1,0:T(8,128)(2,1)S(1)}, u32[]{:S(2)}, u32[]{:S(2)}) collective-permute-start(bf16[1,1,64,512]{3,2,1,0:T(8,128)(2,1)S(1)} %get-tuple-element.13), channel_id=1, source_target_pairs={{1,0},{2,1},{3,2},{4,3},{5,4},{6,5},{7,6},{9,8},{10,9},{11,10},{12... | collective-permute-start | bytes 196616 | tf_op jit(solution)/shard_map/ppermute | solution.py:24
  57.0 6.0 %collective-permute-start = (bf16[1,1,64,512]{3,2,1,0:T(8,128)(2,1)S(1)}, bf16[1,1,64,512]{3,2,1,0:T(8,128)(2,1)S(1)}, u32[]{:S(2)}, u32[]{:S(2)}) collective-permute-start(bf16[1,1,64,512]{3,2,1,0:T(8,128)(2,1)S(1)} %get-tuple-element.12), channel_id=1, source_target_pairs={{0,1},{1,2},{2,3},{3,4},{4,5},{5,6},{6,7},{8,9},{9,10},{10,11},{11... | collective-permute-start | bytes 196616 | tf_op jit(solution)/shard_map/ppermute | solution.py:23
  63.0 6.6 %collective-permute-start.2 = (bf16[1,5,64,512]{3,2,1,0:T(8,128)(2,1)S(1)}, bf16[1,5,64,512]{3,2,1,0:T(8,128)(2,1)S(1)}, u32[]{:S(2)}, u32[]{:S(2)}) collective-permute-start(bf16[1,5,64,512]{3,2,1,0:T(8,128)(2,1)S(1)} %pad_maximum_fusion), channel_id=1, source_target_pairs={{0,8},{8,16},{16,24},{1,9},{9,17},{17,25},{2,10},{10,18},{18,26},{... | collective-permute-start | bytes 983048 | tf_op jit(solution)/shard_map/ppermute | solution.py:13
  69.7 15.1 %collective-permute-start.3 = (bf16[1,5,64,512]{3,2,1,0:T(8,128)(2,1)S(1)}, bf16[1,5,64,512]{3,2,1,0:T(8,128)(2,1)S(1)}, u32[]{:S(2)}, u32[]{:S(2)}) collective-permute-start(bf16[1,5,64,512]{3,2,1,0:T(8,128)(2,1)S(1)} %broadcast_select_fusion.1), channel_id=1, source_target_pairs={{0,8},{8,16},{16,24},{1,9},{9,17},{17,25},{2,10},{10,18},{18,26},{... | collective-permute-start | bytes 983048 | tf_op jit(solution)/shard_map/ppermute | solution.py:13
  122.5 2.6 %copy-start.3 = (f32[512]{0:T(512)S(1)}, f32[512]{0:T(512)}, u32[]{:S(2)}) copy-start(f32[512]{0:T(512)} %param.9) | copy-start | bytes 6148
Sparse Core Ops, SparseCore 0:
  12.8 101.4 all-gather.1
where the time goes:
time: 136 us; the launch traced here: 135 us
  waiting for transfers between devices  43.1 us (32%)
  blocking collectives  40.4 us (30%)
  local copies, waits for them, and re-layouts  21.2 us (16%)
  between operations  13.5 us (10%)
  matrix products  8.36 us (6%)
  starting transfers between devices  7.87 us (6%)
    psum x1, blocking collectives, local(): lax.psum((jnp.sum(grouped, axis=(0, 1, 2, 4)), jnp.sum(grouped * grouped,...  40.4 us
    all_gather x1, waiting for transfers between devices, local(): lax.all_gather(kernel, 'tm', axis=1, tiled=True)  20.4 us
    ppermute x2, waiting for transfers between devices, shifted(): return lax.ppermute(x, axis, pairs)  19.1 us
    unnamed x17, local copies, waits for them, and re-layouts  14 us
    slice x1, local copies, waits for them, and re-layouts, apply_taps(): flat[0]  5.74 us
    dot_general x2, matrix products, apply_taps(): jnp.einsum('fhwc,kc->fhwk', columns[tap_time:tap_time + frames], flat[tap...  5.1 us
    ppermute x1, waiting for transfers between devices, extended_2(): before = lax.ppermute(last, axis, up)  3.54 us
    dot_general x1, matrix products, apply_taps(): jnp.einsum('fhwc,kc->fhwk', columns[0:frames], flat[0], preferred_element...  3.26 us
  transfers between devices with their start and end apart: 5, of which 5 were waited for; matrix products, arithmetic and copies ran while one was open for 7% of the time, Pallas kernels for 0%

commit v1 on v0

--- a/solution.py
+++ b/solution.py
@@ -5,6 +5,11 @@
 
 GROUPS = 32
 EPSILON = 1e-06
+
+
+def gather_blocks(x, name, along):
+    blocks = lax.all_gather(x, name)
+    return jnp.concatenate(blocks, axis=along)
 
 
 def shifted(x, axis, by):
@@ -91,7 +96,7 @@
     cache = jnp.concatenate([minus_two, minus_one], axis=0)
     extended = widen(jnp.concatenate([cache, rimmed], axis=0))
     columns = unfold(extended, height, across)
-    conv = apply_taps(columns, lax.all_gather(kernel, "tm", axis=1, tiled=True), frames)
+    conv = apply_taps(columns, gather_blocks(kernel, "tm", 1), frames)
     return (values + conv + bias).astype(jnp.bfloat16)
 
 

time: 136 us -> 157 us (1.15)
  local copies, waits for them, and re-layouts: 21.2 us -> 41.5 us
  other arithmetic: 0.71 us -> 2.6 us
    all_gather x0 -> x1, local copies, waits for them, and re-layouts: none -> 22.4 us  [gather_blocks(): blocks = lax.all_gather(x, name)]
    unnamed x17 -> x12, local copies, waits for them, and re-layouts: 14 us -> 7.86 us
    slice x1, local copies, waits for them, and re-layouts: 5.74 us -> 9.72 us  [apply_taps(): flat[0]]
    all_gather x1, waiting for transfers between devices: 20.4 us -> 18.2 us  [gather_blocks(): blocks = lax.all_gather(x, name)]
  transfers between devices with their start and end apart: 5 -> 5, of which waited for: 5 -> 5; matrix products, arithmetic and copies ran while one was open for 7% -> 8% of each run, Pallas kernels for 0% -> 0%
where the time goes in v1:
time: 157 us; the launch traced here: 156 us
  waiting for transfers between devices  41.7 us (27%)
  local copies, waits for them, and re-layouts  41.5 us (26%)
  blocking collectives  40.4 us (26%)
  between operations  13.5 us (9%)
  matrix products  8.43 us (5%)
  starting transfers between devices  7.87 us (5%)
  other arithmetic  2.6 us (2%)
    psum x1, blocking collectives, local(): lax.psum((jnp.sum(grouped, axis=(0, 1, 2, 4)), jnp.sum(grouped * grouped,...  40.4 us
    all_gather x1, local copies, waits for them, and re-layouts, gather_blocks(): blocks = lax.all_gather(x, name)  22.4 us
    ppermute x2, waiting for transfers between devices, shifted(): return lax.ppermute(x, axis, pairs)  19.1 us
    all_gather x1, waiting for transfers between devices, gather_blocks(): blocks = lax.all_gather(x, name)  18.2 us
    slice x1, local copies, waits for them, and re-layouts, apply_taps(): flat[0]  9.72 us
    unnamed x12, local copies, waits for them, and re-layouts  7.86 us
    dot_general x2, matrix products, apply_taps(): jnp.einsum('fhwc,kc->fhwk', columns[tap_time:tap_time + frames], flat[tap...  5.15 us
    ppermute x1, waiting for transfers between devices, extended_2(): before = lax.ppermute(last, axis, up)  3.54 us
  transfers between devices with their start and end apart: 5, of which 5 were waited for; matrix products, arithmetic and copies ran while one was open for 8% of the time, Pallas kernels for 0%

profile of v1, /device:TPU:13, one launch (start us, length us, event | category | flops | bytes accessed | tf_op | source)
XLA Modules:
  0.0 156.0 jit_solution(17599423675937550427)
XLA Ops:
  6.5 0.0 all-gather.3.cloned.1.call-start
  6.5 0.7 all-gather.3.cloned.1.call-update
  7.3 1.0 convert_reduce_fusion
  8.3 0.1 reduce_sum.36
  8.3 0.1 reduce_sum.24
  8.4 0.1 reduce_sum.37
  8.5 0.1 reduce_sum.25
  8.7 40.4 %all-reduce.1 = (f32[32]{0:T(128)S(1)}, f32[32]{0:T(128)S(1)}) all-reduce(f32[32]{0:T(128)S(1)} %reduce_sum.37, f32[32]{0:T(128)S(1)} %reduce_sum.25), channel_id=1, replica_groups=mesh['tm'=4,'rows'=8] {'tm','rows'}, use_global_device_ids=true, to_apply=%region_5.6 | all-reduce | flops 64 | bytes 512 | tf_op jit(solution)/shard_map/psum | solution.py:81
  49.0 0.1 mul.43
  49.1 0.1 mul.44
  49.2 0.1 sub.19
  49.3 0.1 sub.20
  49.3 1.1 fusion.26
  50.5 3.0 %collective-permute-start.1 = (bf16[1,1,64,512]{3,2,1,0:T(8,128)(2,1)S(1)}, bf16[1,1,64,512]{3,2,1,0:T(8,128)(2,1)S(1)}, u32[]{:S(2)}, u32[]{:S(2)}) collective-permute-start(bf16[1,1,64,512]{3,2,1,0:T(8,128)(2,1)S(1)} %get-tuple-element.13), channel_id=1, source_target_pairs={{1,0},{2,1},{3,2},{4,3},{5,4},{6,5},{7,6},{9,8},{10,9},{11,10},{12... | collective-permute-start | bytes 196616 | tf_op jit(solution)/shard_map/ppermute | solution.py:29
  53.5 2.3 %collective-permute-start = (bf16[1,1,64,512]{3,2,1,0:T(8,128)(2,1)S(1)}, bf16[1,1,64,512]{3,2,1,0:T(8,128)(2,1)S(1)}, u32[]{:S(2)}, u32[]{:S(2)}) collective-permute-start(bf16[1,1,64,512]{3,2,1,0:T(8,128)(2,1)S(1)} %get-tuple-element.12), channel_id=1, source_target_pairs={{0,1},{1,2},{2,3},{3,4},{4,5},{5,6},{6,7},{8,9},{9,10},{10,11},{11... | collective-permute-start | bytes 196616 | tf_op jit(solution)/shard_map/ppermute | solution.py:28
  55.8 0.1 collective-permute-done.1
  55.9 3.5 %collective-permute-done = bf16[1,1,64,512]{3,2,1,0:T(8,128)(2,1)S(1)} collective-permute-done((bf16[1,1,64,512]{3,2,1,0:T(8,128)(2,1)S(1)}, bf16[1,1,64,512]{3,2,1,0:T(8,128)(2,1)S(1)}, u32[]{:S(2)}, u32[]{:S(2)}) %collective-permute-start) | collective-permute-done | bytes 65568 | tf_op jit(solution)/shard_map/ppermute | solution.py:28
  59.5 1.3 collective-permute-start.2
  60.8 4.9 %collective-permute-done.2 = bf16[1,5,64,512]{3,2,1,0:T(8,128)(2,1)S(1)} collective-permute-done((bf16[1,5,64,512]{3,2,1,0:T(8,128)(2,1)S(1)}, bf16[1,5,64,512]{3,2,1,0:T(8,128)(2,1)S(1)}, u32[]{:S(2)}, u32[]{:S(2)}) %collective-permute-start.2) | collective-permute-done | bytes 327712 | tf_op jit(solution)/shard_map/ppermute | solution.py:18
  65.7 1.3 collective-permute-start.3
  67.0 14.2 %collective-permute-done.3 = bf16[1,5,64,512]{3,2,1,0:T(8,128)(2,1)S(1)} collective-permute-done((bf16[1,5,64,512]{3,2,1,0:T(8,128)(2,1)S(1)}, bf16[1,5,64,512]{3,2,1,0:T(8,128)(2,1)S(1)}, u32[]{:S(2)}, u32[]{:S(2)}) %collective-permute-start.3) | collective-permute-done | bytes 327712 | tf_op jit(solution)/shard_map/ppermute | solution.py:18
  81.2 0.1 broadcast_select_fusion
  81.3 0.1 maximum_maximum_fusion
  81.4 1.0 fusion.12
  82.4 1.0 slice_dynamic-update-slice_fusion.2
  83.4 1.0 fusion.13
  84.4 1.0 fusion.14
  85.4 0.9 slice_dynamic-update-slice_fusion.1
  86.3 1.0 fusion.15
  87.3 1.0 fusion.16
  88.4 0.9 slice_dynamic-update-slice_fusion
  89.3 1.0 fusion.17
  90.3 18.2 %all-gather.3.cloned.1.call-done = bf16[12,128,3,3,512]{4,1,3,2,0:T(8,128)(2,1)} async-done(((bf16[3,128,3,3,512]{4,1,3,2,0:T(8,128)(2,1)}), bf16[12,128,3,3,512]{4,1,3,2,0:T(8,128)(2,1)}) %all-gather.3.cloned.1.call-update) | async-done | bytes 14155792 | tf_op jit(solution)/shard_map/all_gather | solution.py:11
  108.4 22.4 %copy.11 = bf16[4,3,128,3,3,512]{2,0,5,4,3,1:T(4,128)(2,1)} copy(bf16[4,3,128,3,3,512]{5,2,4,3,1,0:T(8,128)(2,1)} %bitcast.86) | data formatting | bytes 28311552 | tf_op jit(solution)/shard_map/all_gather | solution.py:11
  130.9 9.7 %fusion.28 = (bf16[1,4,128,3,3,512]{2,1,5,4,3,0:T(4,128)(2,1)S(1)}, bf16[1,4,128,3,3,512]{2,1,5,4,3,0:T(4,128)(2,1)S(1)}, bf16[1,4,128,3,3,512]{2,1,5,4,3,0:T(4,128)(2,1)S(1)}) fusion(bf16[3,4,128,3,3,512]{2,1,5,4,3,0:T(4,128)(2,1)} %bitcast.85), kind=kLoop, calls=%fused_computation.52 | loop fusion | bytes 28311552 | tf_op jit(solution)/shard_map/slice | solution.py:49
  140.6 2.6 %fusion = f32[3,64,512]{2,1,0:T(8,128)S(1)} fusion(bf16[576,8,4,128]{3,2,1,0:T(4,128)(2,1)S(1)} %bitcast.89, bf16[3,3,64,4608]{3,2,1,0:T(8,128)(2,1)} %fusion.17), kind=kOutput, calls=%fused_computation.1 | convolution fusion | flops 905969664 | bytes 6881280 | tf_op jit(solution)/shard_map/fhwc,kc->fhwk/dot_general | solution.py:52
  143.2 0.0 copy-start
  143.2 0.0 copy-start.1
  143.2 2.6 %fusion.2 = f32[3,64,512]{2,1,0:T(8,128)S(1)} fusion(bf16[576,8,4,128]{3,2,1,0:T(4,128)(2,1)S(1)} %bitcast.88, bf16[3,3,64,4608]{3,2,1,0:T(8,128)(2,1)} %fusion.17), kind=kOutput, calls=%fused_computation.4 | convolution fusion | flops 905969664 | bytes 6881280 | tf_op jit(solution)/shard_map/fhwc,kc->fhwk/dot_general | solution.py:52
  145.8 0.0 copy-done
  145.8 0.0 copy-done.1
  145.8 3.3 %fusion.11 = bf16[1,3,64,512]{3,2,1,0:T(8,128)(2,1)} fusion(f32[3,64,512]{2,1,0:T(8,128)S(1)} %fusion, f32[3,64,512]{2,1,0:T(8,128)S(1)} %fusion.2, bf16[576,8,4,128]{3,2,1,0:T(4,128)(2,1)S(1)} %bitcast.87, bf16[3,3,64,4608]{3,2,1,0:T(8,128)(2,1)} %fusion.17, bf16[1,3,64,512]{3,2,1,0:T(8,128)(2,1)S(1)} %copy-done, f32[512]{0:T(512)S(1)} %copy-done.1), kind=kOutput, calls=%fused_computation.17 | convolution fusion | flops 906559488 | bytes 7669760 | tf_op jit(solution)/shard_map/fhwc,kc->fhwk/dot_general | solution.py:48
  (4 shorter events, 0.1 us)
Async XLA Ops:
  6.5 101.9 %all-gather.3.cloned.1.call-start = ((), (), s32[]{:S(2)}) async-start(), calls=%async_computation | async-start | bytes 17694720 | tf_op jit(solution)/shard_map/all_gather | solution.py:11
  50.5 5.4 %collective-permute-start.1 = (bf16[1,1,64,512]{3,2,1,0:T(8,128)(2,1)S(1)}, bf16[1,1,64,512]{3,2,1,0:T(8,128)(2,1)S(1)}, u32[]{:S(2)}, u32[]{:S(2)}) collective-permute-start(bf16[1,1,64,512]{3,2,1,0:T(8,128)(2,1)S(1)} %get-tuple-element.13), channel_id=1, source_target_pairs={{1,0},{2,1},{3,2},{4,3},{5,4},{6,5},{7,6},{9,8},{10,9},{11,10},{12... | collective-permute-start | bytes 196616 | tf_op jit(solution)/shard_map/ppermute | solution.py:29
  53.5 6.0 %collective-permute-start = (bf16[1,1,64,512]{3,2,1,0:T(8,128)(2,1)S(1)}, bf16[1,1,64,512]{3,2,1,0:T(8,128)(2,1)S(1)}, u32[]{:S(2)}, u32[]{:S(2)}) collective-permute-start(bf16[1,1,64,512]{3,2,1,0:T(8,128)(2,1)S(1)} %get-tuple-element.12), channel_id=1, source_target_pairs={{0,1},{1,2},{2,3},{3,4},{4,5},{5,6},{6,7},{8,9},{9,10},{10,11},{11... | collective-permute-start | bytes 196616 | tf_op jit(solution)/shard_map/ppermute | solution.py:28
  59.5 6.2 %collective-permute-start.2 = (bf16[1,5,64,512]{3,2,1,0:T(8,128)(2,1)S(1)}, bf16[1,5,64,512]{3,2,1,0:T(8,128)(2,1)S(1)}, u32[]{:S(2)}, u32[]{:S(2)}) collective-permute-start(bf16[1,5,64,512]{3,2,1,0:T(8,128)(2,1)S(1)} %pad_maximum_fusion), channel_id=1, source_target_pairs={{0,8},{8,16},{16,24},{1,9},{9,17},{17,25},{2,10},{10,18},{18,26},{... | collective-permute-start | bytes 983048 | tf_op jit(solution)/shard_map/ppermute | solution.py:18
  65.7 15.5 %collective-permute-start.3 = (bf16[1,5,64,512]{3,2,1,0:T(8,128)(2,1)S(1)}, bf16[1,5,64,512]{3,2,1,0:T(8,128)(2,1)S(1)}, u32[]{:S(2)}, u32[]{:S(2)}) collective-permute-start(bf16[1,5,64,512]{3,2,1,0:T(8,128)(2,1)S(1)} %broadcast_select_fusion.1), channel_id=1, source_target_pairs={{0,8},{8,16},{16,24},{1,9},{9,17},{17,25},{2,10},{10,18},{18,26},{... | collective-permute-start | bytes 983048 | tf_op jit(solution)/shard_map/ppermute | solution.py:18
  143.2 2.6 %copy-start = (bf16[1,3,64,512]{3,2,1,0:T(8,128)(2,1)S(1)}, bf16[1,3,64,512]{3,2,1,0:T(8,128)(2,1)}, u32[]{:S(2)}) copy-start(bf16[1,3,64,512]{3,2,1,0:T(8,128)(2,1)} %param.5) | copy-start | bytes 589828
  143.2 2.6 %copy-start.1 = (f32[512]{0:T(512)S(1)}, f32[512]{0:T(512)}, u32[]{:S(2)}) copy-start(f32[512]{0:T(512)} %param.9) | copy-start | bytes 6148
Sparse Core Ops, SparseCore 0:
  8.9 99.5 all-gather.2
